TPU v7x, 32 devices: a whole 2x2x4 slice. The times are simulated.
32 devices in a mesh: rows: 8 (over y, x, core), cols: 4 (over z).
Axes of the slice: x: 2, y: 2, z: 4, core: 2. Of those that a mesh axis runs over, the one named last changes fastest.
Arguments:
- intensity: float32 [4096, 4096], P('rows', 'cols'), may hold values from -0.5 to 1.5, as said below
- edge_weight: float32 [4096, 4096], P('rows', 'cols'), may hold values from 0.2 to 2
- labels: int32 [4096, 4096], P('rows', 'cols'), may hold values from 0 to 1
- tile_cost: int32 [16, 16], replicated, may hold values from 0 to 3, as said below
- tile_owner: int32 [16, 16], replicated, may hold values from -1 to 31, as said below
Outputs:
- slot_field: float32 [32, 4, 256, 256], P('rows', 'cols')
Inputs may be any that keep to these rules, and one draw needn't show every extreme that they name: `intensity`: intensity of stained tissue. `tile_cost`: 0 marks a background tile, 1 to 3 a tissue tile. `tile_owner`: -1 exactly for background tiles. A tissue tile's value is k * 4 + s: it goes to slot s of the device with rows index k in its own column band; within one band no two tiles share a value; the tiles of one device's block send at most 1 tile to any one device, and in every draw some block sends exactly 1 to one device and some device receives all 4 of its slots filled.
All inputs are finite; a program needn't handle non-finite values.
Results may differ from a plain program's by a relative error of at most 0.0001.
Values sent between devices are 32-bit elements; how exact they have to be, the bound alone decides.
A program may use at most 128 MiB of HBM per device.

v0:
```python
import jax
import jax.numpy as jnp
from jax import lax
from jax.sharding import PartitionSpec as P

TILE = 256
ITERS_BEFORE = 2
ITERS_AFTER = 2


sigma_step = 0.35
tau_step = 0.35
fidelity = 1.0


def from_behind(x, axis, by):
    peers = lax.axis_size(axis)
    pairs = [(i, i + by) for i in range(peers) if 0 <= i + by < peers]
    return lax.ppermute(x, axis, pairs)


def split_tiles(block, tile_side):
    height = block.shape[-2]
    span_cols = block.shape[-1]
    leading = block.shape[:-2]
    lead_count = len(leading)
    shaped = block.reshape(
        leading + (height // tile_side, tile_side, span_cols // tile_side, tile_side)
    )
    axes_order = tuple(range(lead_count)) + (
        lead_count,
        lead_count + 2,
        lead_count + 1,
        lead_count + 3,
    )
    tiled = shaped.transpose(axes_order)
    return tiled.reshape(
        leading + (height // tile_side * (span_cols // tile_side), tile_side, tile_side)
    )


def project(flux_down, flux_right, grad_down, grad_right, edge_weight):
    trial_down = flux_down + sigma_step * grad_down
    trial_right = flux_right + sigma_step * grad_right
    length = jnp.sqrt(trial_down * trial_down + trial_right * trial_right)
    shrink = jnp.maximum(1.0, length / edge_weight)
    return (trial_down / shrink, trial_right / shrink)


def region_term(intensity, totals):
    mean_in = totals[0] / totals[1]
    mean_out = totals[2] / totals[3]
    return (intensity - mean_in) ** 2 - (intensity - mean_out) ** 2


def grid_step(
    relaxed,
    extrapolated,
    flux_down,
    flux_right,
    intensity,
    edge_weight,
    weight_cells,
    frozen,
    keep_down,
    keep_right,
):
    totals = lax.psum(
        (
            jnp.sum(relaxed * intensity),
            jnp.sum(relaxed),
            jnp.sum((1.0 - relaxed) * intensity),
            jnp.sum(1.0 - relaxed),
        ),
        ("rows", "cols"),
    )
    region = region_term(intensity, totals)
    leading = extrapolated if frozen is None else jnp.where(frozen, relaxed, extrapolated)
    below_rim = from_behind(leading[:1], "rows", -1)
    beyond_rim = from_behind(leading[:, 0][None, :], "cols", -1)
    grad_down = (jnp.concatenate([leading[1:], below_rim], axis=0) - leading) * keep_down
    grad_right = (jnp.concatenate([leading[:, 1:], beyond_rim.T], axis=1) - leading) * keep_right
    new_down, new_right = project(flux_down, flux_right, grad_down, grad_right, edge_weight)
    if frozen is not None:
        new_down = jnp.where(frozen, flux_down, new_down)
        new_right = jnp.where(frozen, flux_right, new_right)
    above_rim = from_behind(new_down[-1:], "rows", 1)
    before_rim = from_behind(new_right[:, -1][None, :], "cols", 1)
    spread = new_down - jnp.concatenate([above_rim, new_down[:-1]], axis=0)
    spread = spread + new_right - jnp.concatenate([before_rim.T, new_right[:, :-1]], axis=1)
    updated = jnp.clip(relaxed + tau_step * (spread - weight_cells * region), 0.0, 1.0)
    if frozen is not None:
        updated = jnp.where(frozen, relaxed, updated)
    return (updated, 2.0 * updated - relaxed, new_down, new_right)


def pack_tiles(tile_set, local_owner, target_rows, capacity, slots_dev):
    target = jnp.where(local_owner >= 0, local_owner // slots_dev, -1)
    positions = jnp.arange(local_owner.shape[0], dtype=jnp.int32)
    earlier_same = (target[:, None] == target[None, :]) & (positions[None, :] < positions[:, None])
    order_rank = jnp.sum(earlier_same.astype(jnp.int32), axis=1)
    position = jnp.where(target >= 0, target * capacity + order_rank, -1)
    wanted = jnp.arange(target_rows * capacity, dtype=jnp.int32)
    matches = position[None, :] == wanted[:, None]
    source = jnp.sum(jnp.where(matches, positions[None, :], 0), axis=1)
    filled = jnp.any(matches, axis=1).astype(tile_set.dtype)
    packed = tile_set[source] * filled[:, None, None, None]
    return packed.reshape((target_rows, capacity) + tile_set.shape[1:])


def unpack_tiles(received, stripe_owner, row_index, slots_dev, tiles_dev):
    positions = jnp.arange(stripe_owner.shape[0], dtype=jnp.int32)
    own_slots = row_index * slots_dev + jnp.arange(slots_dev, dtype=jnp.int32)
    owner_hit = stripe_owner[None, :] == own_slots[:, None]
    tile_of = jnp.sum(jnp.where(owner_hit, positions[None, :], 0), axis=1)
    occupied_mask = jnp.any(owner_hit, axis=1)
    source = tile_of // tiles_dev
    target = jnp.where(stripe_owner >= 0, stripe_owner // slots_dev, -1)
    earlier = (
        (positions[None, :] // tiles_dev == source[:, None])
        & (target[None, :] == row_index)
        & (positions[None, :] < tile_of[:, None])
    )
    order_rank = jnp.sum(earlier.astype(jnp.int32), axis=1)
    picked = (
        received[source, order_rank] * occupied_mask.astype(received.dtype)[:, None, None, None]
    )
    return (picked, tile_of, occupied_mask)


def body(intensity, edge_weight, labels, tile_cost, tile_owner):
    block_rows, block_cols = intensity.shape
    tiles_down = block_rows // TILE
    tiles_across = block_cols // TILE
    tiles_dev = tiles_down * tiles_across
    slots_dev = tiles_dev // 2
    row_index = lax.axis_index("rows")
    col_index = lax.axis_index("cols")
    row_count = lax.axis_size("rows")
    col_count = lax.axis_size("cols")
    capacity = -(-tiles_dev // row_count)
    cost_block = lax.dynamic_slice(
        tile_cost, (row_index * tiles_down, col_index * tiles_across), (tiles_down, tiles_across)
    )
    cost_cells = jnp.broadcast_to(
        cost_block[:, None, :, None], (tiles_down, TILE, tiles_across, TILE)
    ).reshape(block_rows, block_cols)
    weight_cells = fidelity * cost_cells.astype(jnp.float32)
    background = cost_cells == 0
    global_rows = row_index * block_rows + jnp.arange(block_rows, dtype=jnp.int32)
    global_cols = col_index * block_cols + jnp.arange(block_cols, dtype=jnp.int32)
    keep_down = (global_rows != row_count * block_rows - 1).astype(jnp.float32)[:, None]
    keep_right = (global_cols != col_count * block_cols - 1).astype(jnp.float32)[None, :]
    relaxed = labels.astype(jnp.float32)
    extrapolated = relaxed
    flux_down = jnp.zeros_like(relaxed)
    flux_right = jnp.zeros_like(relaxed)
    grid_sweeps = ITERS_BEFORE + ITERS_AFTER
    for iteration in range(grid_sweeps):
        frozen = background if iteration >= ITERS_BEFORE else None
        relaxed, extrapolated, flux_down, flux_right = grid_step(
            relaxed,
            extrapolated,
            flux_down,
            flux_right,
            intensity,
            edge_weight,
            weight_cells,
            frozen,
            keep_down,
            keep_right,
        )
    stripe_owner = lax.dynamic_slice_in_dim(
        tile_owner, col_index * tiles_across, tiles_across, 1
    ).reshape(-1)
    local_owner = lax.dynamic_slice_in_dim(stripe_owner, row_index * tiles_dev, tiles_dev, 0)
    tile_set = split_tiles(relaxed[None], TILE).transpose(1, 0, 2, 3)
    packed = pack_tiles(tile_set, local_owner, row_count, capacity, slots_dev)
    received = lax.all_to_all(packed, "rows", split_axis=0, concat_axis=0, tiled=True)
    picked, tile_of, occupied_mask = unpack_tiles(
        received, stripe_owner, row_index, slots_dev, tiles_dev
    )
    return picked


def solution(mesh):
    return jax.shard_map(
        body,
        mesh=mesh,
        in_specs=(P("rows", "cols"), P("rows", "cols"), P("rows", "cols"), P(), P()),
        out_specs=P("rows", "cols", None, None),
        check_vma=False,
    )
```

profile of v0, /device:TPU:1, one launch (start us, length us, event | category | flops | bytes accessed | tf_op | source)
XLA Modules:
  0.0 341.0 jit_solution(8632451200485779739)
XLA Ops:
  5.7 3.5 %slice.132 = f32[511,1024]{1,0:T(8,128)} slice(f32[512,1024]{1,0:T(8,128)} %copy-done.18), slice={[1:512], [0:1024]} | slice | bytes 4186112 | tf_op jit(solution)/shard_map/slice | solution.py:81
  11.2 6.0 %fusion.52 = (f32[512,1024]{1,0:T(8,128)S(1)}, f32[512,1024]{1,0:T(8,128)S(1)}, f32[]{:T(128)}, f32[]{:T(128)}, f32[]{:T(128)}, /*index=5*/f32[]{:T(128)}) fusion(f32[512,1024]{1,0:T(8,128)} %param.6, f32[1024]{0:T(1024)S(1)} %fusion.55, f32[512,1]{1,0:T(8,128)S(1)} %copy.36, f32[512,1023]{1,0:T(8,128)} %slice.134, f32[512]{0:T(512)S(1)} %fusion.58, ...), kind=kLoop, calls=%fused_computation.86 | loop fusion | flops 12058620 | bytes 14686224 | tf_op jit(solution)/shard_map/div | solution.py:47
  17.5 5.3 %collective-permute-start.3 = (f32[1,512]{1,0:T(1,128)S(1)}, f32[1,512]{1,0:T(1,128)S(1)}, u32[]{:S(2)}, u32[]{:S(2)}) collective-permute-start(f32[1,512]{1,0:T(1,128)S(1)} %bitcast.95), channel_id=1, source_target_pairs={{0,1},{1,2},{2,3},{4,5},{5,6},{6,7},{8,9},{9,10},{10,11},{12,13},{... | collective-permute-start | bytes 6152 | tf_op jit(solution)/shard_map/ppermute | solution.py:19
  22.8 3.7 %collective-permute-start.2 = (f32[1,1024]{1,0:T(1,128)S(1)}, f32[1,1024]{1,0:T(1,128)S(1)}, u32[]{:S(2)}, u32[]{:S(2)}) collective-permute-start(f32[1,1024]{1,0:T(1,128)S(1)} %slice.136), channel_id=1, source_target_pairs={{0,4},{4,8},{8,12},{12,16},{16,20},{20,24},{24,28},{1,5},{5,9},{9,... | collective-permute-start | bytes 12296 | tf_op jit(solution)/shard_map/ppermute | solution.py:19
  28.2 39.1 %all-reduce.3 = (f32[]{:T(128)}, f32[]{:T(128)}, f32[]{:T(128)}, f32[]{:T(128)}) all-reduce(f32[]{:T(128)} %get-tuple-element.57, f32[]{:T(128)} %get-tuple-element.55, f32[]{:T(128)} %get-tuple-element.58, f32[]{:T(128)} %get-tuple-element.56), channel_id=1, replica_groups=mesh['rows'=8,'cols'=4] {'rows','cols'}, use_global_device_ids=true, to_apply=%region_5.0 | all-reduce | flops 4 | bytes 32 | tf_op jit(solution)/shard_map/psum | solution.py:68
  70.1 6.6 %fusion.70 = (f32[]{:T(128)}, f32[]{:T(128)}, f32[]{:T(128)}, f32[]{:T(128)}, f32[512,1024]{1,0:T(8,128)S(1)}) fusion(f32[512,1024]{1,0:T(8,128)} %param.5, f32[512,1024]{1,0:T(8,128)S(1)} %bitcast.67, f32[]{:T(128)S(6)} %div.116, f32[]{:T(128)S(6)} %div.115, f32[512,1023]{1,0:T(8,128)} %bitcast.71, f32[512,1]{1,0:T(8,128)S(1)} %copy.37, ...), kind=kLoop, calls=%fused_computation.160 | loop fusion | flops 12058620 | bytes 16777240 | tf_op jit(solution)/shard_map/reduce_sum | solution.py:71
  86.4 6.1 %fusion.50 = (f32[512,1024]{1,0:T(8,128)S(1)}, f32[512,1024]{1,0:T(8,128)S(1)}, f32[512,1024]{1,0:T(8,128)S(1)}) fusion(f32[512,1024]{1,0:T(8,128)} %param.6, f32[512,1024]{1,0:T(8,128)} %copy-done.11, f32[512]{0:T(512)S(1)} %fusion.58, f32[512,1024]{1,0:T(8,128)} %copy-done.4, f32[1,1024]{1,0:T(1,128)S(1)} %collective-permute-done.4, ...), kind=kLoop, calls=%fused_computation.80 | loop fusion | flops 8388608 | bytes 18880512 | tf_op jit(solution)/shard_map/div | solution.py:47
  95.1 4.3 %collective-permute-start.7 = (f32[1,512]{1,0:T(1,128)S(1)}, f32[1,512]{1,0:T(1,128)S(1)}, u32[]{:S(2)}, u32[]{:S(2)}) collective-permute-start(f32[1,512]{1,0:T(1,128)S(1)} %bitcast.92), channel_id=1, source_target_pairs={{0,1},{1,2},{2,3},{4,5},{5,6},{6,7},{8,9},{9,10},{10,11},{12,13},{... | collective-permute-start | bytes 6152 | tf_op jit(solution)/shard_map/ppermute | solution.py:19
  99.4 4.1 %collective-permute-start.6 = (f32[1,1024]{1,0:T(1,128)S(1)}, f32[1,1024]{1,0:T(1,128)S(1)}, u32[]{:S(2)}, u32[]{:S(2)}) collective-permute-start(f32[1,1024]{1,0:T(1,128)S(1)} %slice.144), channel_id=1, source_target_pairs={{0,4},{4,8},{8,12},{12,16},{16,20},{20,24},{24,28},{1,5},{5,9},{9,... | collective-permute-start | bytes 12296 | tf_op jit(solution)/shard_map/ppermute | solution.py:19
  104.9 37.4 %all-reduce.2 = (f32[]{:T(128)}, f32[]{:T(128)}, f32[]{:T(128)}, f32[]{:T(128)}) all-reduce(f32[]{:T(128)} %get-tuple-element.23, f32[]{:T(128)} %get-tuple-element.22, f32[]{:T(128)} %get-tuple-element.24, f32[]{:T(128)} %get-tuple-element.21), channel_id=1, replica_groups=mesh['rows'=8,'cols'=4] {'rows','cols'}, use_global_device_ids=true, to_apply=%region_13.14 | all-reduce | flops 4 | bytes 32 | tf_op jit(solution)/shard_map/psum | solution.py:68
  145.1 7.3 %fusion.69 = (f32[]{:T(128)}, f32[]{:T(128)}, f32[]{:T(128)}, f32[]{:T(128)}, f32[512,1024]{1,0:T(8,128)S(1)}) fusion(f32[512,1024]{1,0:T(8,128)} %param.5, f32[512,1024]{1,0:T(8,128)} %copy-done.13, f32[512,1024]{1,0:T(8,128)S(1)} %bitcast.68, f32[]{:T(128)S(6)} %div.121, f32[]{:T(128)S(6)} %div.120, f32[512,1023]{1,0:T(8,128)} %bitcast.72, ...), kind=kLoop, calls=%fused_computation.159 | loop fusion | flops 11534332 | bytes 16777240 | tf_op jit(solution)/shard_map/reduce_sum | solution.py:71
  162.2 6.1 %divide_select_fusion.3 = (f32[512,1024]{1,0:T(8,128)S(1)}, f32[512,1024]{1,0:T(8,128)S(1)}) fusion(pred[512,1024]{1,0:T(8,128)(4,1)S(1)} %bitcast.78, f32[512,1024]{1,0:T(8,128)} %copy-done.10, f32[512,1024]{1,0:T(8,128)} %param.6, f32[512,1024]{1,0:T(8,128)} %copy-done.8, f32[1024]{0:T(1024)S(1)} %fusion.55, f32[512,1024]{1,0:T(8,128)} %copy-done.6, ...), kind=kLoop, calls=%fused_computation.73 | loop fusion | flops 9961472 | bytes 17307648 | tf_op jit(solution)/shard_map/jit(_where)/select_n | solution.py:85
  169.8 4.3 %collective-permute-start.11 = (f32[1,512]{1,0:T(1,128)S(1)}, f32[1,512]{1,0:T(1,128)S(1)}, u32[]{:S(2)}, u32[]{:S(2)}) collective-permute-start(f32[1,512]{1,0:T(1,128)S(1)} %bitcast.98), channel_id=1, source_target_pairs={{0,1},{1,2},{2,3},{4,5},{5,6},{6,7},{8,9},{9,10},{10,11},{12,13},{... | collective-permute-start | bytes 6152 | tf_op jit(solution)/shard_map/ppermute | solution.py:19
  174.1 4.1 %collective-permute-start.10 = (f32[1,1024]{1,0:T(1,128)S(1)}, f32[1,1024]{1,0:T(1,128)S(1)}, u32[]{:S(2)}, u32[]{:S(2)}) collective-permute-start(f32[1,1024]{1,0:T(1,128)S(1)} %slice.152), channel_id=1, source_target_pairs={{0,4},{4,8},{8,12},{12,16},{16,20},{20,24},{24,28},{1,5},{5,9},{9,... | collective-permute-start | bytes 12296 | tf_op jit(solution)/shard_map/ppermute | solution.py:19
  178.2 38.7 %all-reduce.1 = (f32[]{:T(128)}, f32[]{:T(128)}, f32[]{:T(128)}, f32[]{:T(128)}) all-reduce(f32[]{:T(128)} %get-tuple-element.19, f32[]{:T(128)} %get-tuple-element.18, f32[]{:T(128)} %get-tuple-element.20, f32[]{:T(128)} %get-tuple-element.17), channel_id=1, replica_groups=mesh['rows'=8,'cols'=4] {'rows','cols'}, use_global_device_ids=true, to_apply=%region_21.22 | all-reduce | flops 4 | bytes 32 | tf_op jit(solution)/shard_map/psum | solution.py:68
  219.7 7.5 %fusion.68 = (f32[]{:T(128)}, f32[]{:T(128)}, f32[]{:T(128)}, f32[]{:T(128)}, f32[512,1024]{1,0:T(8,128)S(1)}) fusion(f32[512,1024]{1,0:T(8,128)} %param.5, pred[512,1024]{1,0:T(8,128)(4,1)S(1)} %bitcast.79, f32[512,1024]{1,0:T(8,128)} %copy-done.16, f32[512,1024]{1,0:T(8,128)S(1)} %bitcast.69, f32[]{:T(128)S(6)} %div.126, f32[]{:T(128)S(6)} %div.125, ...), kind=kLoop, calls=%fused_computation.158 | loop fusion | flops 12058620 | bytes 17301528 | tf_op jit(solution)/shard_map/reduce_sum | solution.py:71
  229.9 3.2 collective-permute-start.12
  236.9 6.1 %divide_select_fusion.1 = (f32[512,1024]{1,0:T(8,128)S(1)}, f32[512,1024]{1,0:T(8,128)S(1)}) fusion(pred[512,1024]{1,0:T(8,128)(4,1)S(1)} %bitcast.81, f32[512,1024]{1,0:T(8,128)} %copy-done.12, f32[512,1024]{1,0:T(8,128)} %param.6, f32[512,1024]{1,0:T(8,128)} %copy-done.9, f32[1024]{0:T(1024)S(1)} %fusion.55, f32[512,1024]{1,0:T(8,128)} %copy-done.5, ...), kind=kLoop, calls=%fused_computation.67 | loop fusion | flops 9961472 | bytes 17307648 | tf_op jit(solution)/shard_map/jit(_where)/select_n | solution.py:85
  244.6 4.3 %collective-permute-start.15 = (f32[1,512]{1,0:T(1,128)S(1)}, f32[1,512]{1,0:T(1,128)S(1)}, u32[]{:S(2)}, u32[]{:S(2)}) collective-permute-start(f32[1,512]{1,0:T(1,128)S(1)} %bitcast.96), channel_id=1, source_target_pairs={{0,1},{1,2},{2,3},{4,5},{5,6},{6,7},{8,9},{9,10},{10,11},{12,13},{... | collective-permute-start | bytes 6152 | tf_op jit(solution)/shard_map/ppermute | solution.py:19
  248.9 4.1 %collective-permute-start.14 = (f32[1,1024]{1,0:T(1,128)S(1)}, f32[1,1024]{1,0:T(1,128)S(1)}, u32[]{:S(2)}, u32[]{:S(2)}) collective-permute-start(f32[1,1024]{1,0:T(1,128)S(1)} %slice.160), channel_id=1, source_target_pairs={{0,4},{4,8},{8,12},{12,16},{16,20},{20,24},{24,28},{1,5},{5,9},{9,... | collective-permute-start | bytes 12296 | tf_op jit(solution)/shard_map/ppermute | solution.py:19
  253.1 37.4 %all-reduce = (f32[]{:T(128)}, f32[]{:T(128)}, f32[]{:T(128)}, f32[]{:T(128)}) all-reduce(f32[]{:T(128)} %get-tuple-element.15, f32[]{:T(128)} %get-tuple-element.14, f32[]{:T(128)} %get-tuple-element.16, f32[]{:T(128)} %get-tuple-element.13), channel_id=1, replica_groups=mesh['rows'=8,'cols'=4] {'rows','cols'}, use_global_device_ids=true, to_apply=%region_29.30 | all-reduce | flops 4 | bytes 32 | tf_op jit(solution)/shard_map/psum | solution.py:68
  293.2 8.0 %fusion.47 = f32[512,1024]{1,0:T(8,128)} fusion(pred[512,1024]{1,0:T(8,128)(4,1)S(1)} %bitcast.82, f32[512,1024]{1,0:T(8,128)} %copy-done.22, f32[512,1024]{1,0:T(8,128)} %copy-done.20, f32[512,1024]{1,0:T(8,128)} %copy-done.21, f32[511,1024]{1,0:T(8,128)} %bitcast.84, f32[1,1024]{1,0:T(1,128)S(1)} %collective-permute-done.14, f32[512,1023]{1,0:T(8,128)} %bitcast.83, ...), kind=kLoop, calls=%fused_computation.61 | loop fusion | flops 8388608 | bytes 17301512 | tf_op jit(solution)/shard_map/jit(_where)/select_n | solution.py:93
  309.0 5.5 %all-to-all-start = ((f32[8,1,1,256,256]{4,3,2,1,0:T(8,128)}), f32[8,1,1,256,256]{4,3,2,1,0:T(8,128)}, u32[]{:S(2)}, u32[]{:S(2)}) async-start(f32[8,1,1,256,256]{4,3,2,1,0:T(8,128)} %fusion.48), calls=%async_computation | async-start | bytes 4194304 | tf_op jit(solution)/shard_map/all_to_all | solution.py:179
  315.1 22.5 %all-to-all-done = f32[8,1,1,256,256]{4,3,2,1,0:T(8,128)} async-done(((f32[8,1,1,256,256]{4,3,2,1,0:T(8,128)}), f32[8,1,1,256,256]{4,3,2,1,0:T(8,128)}, u32[]{:S(2)}, u32[]{:S(2)}) %all-to-all-start) | async-done | bytes 2097184 | tf_op jit(solution)/shard_map/all_to_all | solution.py:179
  (138 shorter events, 55.0 us)
Async XLA Ops:
  1.9 9.1 %collective-permute-start.1 = (f32[1,512]{1,0:T(1,128)S(1)}, f32[1,512]{1,0:T(1,128)S(1)}, u32[]{:S(2)}, u32[]{:S(2)}) collective-permute-start(f32[1,512]{1,0:T(1,128)S(1)} %bitcast.90), channel_id=1, source_target_pairs={{1,0},{2,1},{3,2},{5,4},{6,5},{7,6},{9,8},{10,9},{11,10},{13,12},{... | collective-permute-start | bytes 6152 | tf_op jit(solution)/shard_map/ppermute | solution.py:19
  3.3 8.0 %collective-permute-start = (f32[1,1024]{1,0:T(1,128)S(1)}, f32[1,1024]{1,0:T(1,128)S(1)}, u32[]{:S(2)}, u32[]{:S(2)}) collective-permute-start(f32[1,1024]{1,0:T(1,128)S(1)} %slice.133), channel_id=1, source_target_pairs={{4,0},{8,4},{12,8},{16,12},{20,16},{24,20},{28,24},{5,1},{9,5},{13... | collective-permute-start | bytes 12296 | tf_op jit(solution)/shard_map/ppermute | solution.py:19
  17.3 10.9 %copy-start.7 = (f32[512,1024]{1,0:T(8,128)}, f32[512,1024]{1,0:T(8,128)S(1)}, u32[]{:S(2)}) copy-start(f32[512,1024]{1,0:T(8,128)S(1)} %get-tuple-element.54) | copy-start | bytes 6291460
  17.3 10.9 %copy-start.11 = (f32[512,1024]{1,0:T(8,128)}, f32[512,1024]{1,0:T(8,128)S(1)}, u32[]{:S(2)}) copy-start(f32[512,1024]{1,0:T(8,128)S(1)} %get-tuple-element.53) | copy-start | bytes 6291460
  17.5 52.4 %collective-permute-start.3 = (f32[1,512]{1,0:T(1,128)S(1)}, f32[1,512]{1,0:T(1,128)S(1)}, u32[]{:S(2)}, u32[]{:S(2)}) collective-permute-start(f32[1,512]{1,0:T(1,128)S(1)} %bitcast.95), channel_id=1, source_target_pairs={{0,1},{1,2},{2,3},{4,5},{5,6},{6,7},{8,9},{9,10},{10,11},{12,13},{... | collective-permute-start | bytes 6152 | tf_op jit(solution)/shard_map/ppermute | solution.py:19
  22.8 47.2 %collective-permute-start.2 = (f32[1,1024]{1,0:T(1,128)S(1)}, f32[1,1024]{1,0:T(1,128)S(1)}, u32[]{:S(2)}, u32[]{:S(2)}) collective-permute-start(f32[1,1024]{1,0:T(1,128)S(1)} %slice.136), channel_id=1, source_target_pairs={{0,4},{4,8},{8,12},{12,16},{16,20},{20,24},{24,28},{1,5},{5,9},{9,... | collective-permute-start | bytes 12296 | tf_op jit(solution)/shard_map/ppermute | solution.py:19
  70.1 6.6 %copy-start.15 = (s32[512,1024]{1,0:T(8,128)S(1)}, s32[512,1024]{1,0:T(8,128)}, u32[]{:S(2)}) copy-start(s32[512,1024]{1,0:T(8,128)} %param.7) | copy-start | bytes 6291460
  77.9 6.4 %copy-start.4 = (f32[512,1024]{1,0:T(8,128)}, f32[512,1024]{1,0:T(8,128)S(1)}, u32[]{:S(2)}) copy-start(f32[512,1024]{1,0:T(8,128)S(1)} %multiply_subtract_fusion) | copy-start | bytes 6291460
  78.1 8.1 %collective-permute-start.5 = (f32[1,512]{1,0:T(1,128)S(1)}, f32[1,512]{1,0:T(1,128)S(1)}, u32[]{:S(2)}, u32[]{:S(2)}) collective-permute-start(f32[1,512]{1,0:T(1,128)S(1)} %bitcast.99), channel_id=1, source_target_pairs={{1,0},{2,1},{3,2},{5,4},{6,5},{7,6},{9,8},{10,9},{11,10},{13,12},{... | collective-permute-start | bytes 6152 | tf_op jit(solution)/shard_map/ppermute | solution.py:19
  79.4 7.0 %collective-permute-start.4 = (f32[1,1024]{1,0:T(1,128)S(1)}, f32[1,1024]{1,0:T(1,128)S(1)}, u32[]{:S(2)}, u32[]{:S(2)}) collective-permute-start(f32[1,1024]{1,0:T(1,128)S(1)} %slice.141), channel_id=1, source_target_pairs={{4,0},{8,4},{12,8},{16,12},{20,16},{24,20},{28,24},{5,1},{9,5},{13... | collective-permute-start | bytes 12296 | tf_op jit(solution)/shard_map/ppermute | solution.py:19
  92.5 6.9 %copy-start.10 = (f32[512,1024]{1,0:T(8,128)}, f32[512,1024]{1,0:T(8,128)S(1)}, u32[]{:S(2)}) copy-start(f32[512,1024]{1,0:T(8,128)S(1)} %get-tuple-element.46) | copy-start | bytes 6291460
  95.1 49.8 %collective-permute-start.7 = (f32[1,512]{1,0:T(1,128)S(1)}, f32[1,512]{1,0:T(1,128)S(1)}, u32[]{:S(2)}, u32[]{:S(2)}) collective-permute-start(f32[1,512]{1,0:T(1,128)S(1)} %bitcast.92), channel_id=1, source_target_pairs={{0,1},{1,2},{2,3},{4,5},{5,6},{6,7},{8,9},{9,10},{10,11},{12,13},{... | collective-permute-start | bytes 6152 | tf_op jit(solution)/shard_map/ppermute | solution.py:19
  99.4 45.7 %collective-permute-start.6 = (f32[1,1024]{1,0:T(1,128)S(1)}, f32[1,1024]{1,0:T(1,128)S(1)}, u32[]{:S(2)}, u32[]{:S(2)}) collective-permute-start(f32[1,1024]{1,0:T(1,128)S(1)} %slice.144), channel_id=1, source_target_pairs={{0,4},{4,8},{8,12},{12,16},{16,20},{20,24},{24,28},{1,5},{5,9},{9,... | collective-permute-start | bytes 12296 | tf_op jit(solution)/shard_map/ppermute | solution.py:19
  145.1 7.3 %copy-start.14 = (f32[512,1024]{1,0:T(8,128)S(1)}, f32[512,1024]{1,0:T(8,128)}, u32[]{:S(2)}) copy-start(f32[512,1024]{1,0:T(8,128)} %copy-done.13) | copy-start | bytes 6291460
  153.9 8.1 %collective-permute-start.9 = (f32[1,512]{1,0:T(1,128)S(1)}, f32[1,512]{1,0:T(1,128)S(1)}, u32[]{:S(2)}, u32[]{:S(2)}) collective-permute-start(f32[1,512]{1,0:T(1,128)S(1)} %bitcast.103), channel_id=1, source_target_pairs={{1,0},{2,1},{3,2},{5,4},{6,5},{7,6},{9,8},{10,9},{11,10},{13,12},{... | collective-permute-start | bytes 6152 | tf_op jit(solution)/shard_map/ppermute | solution.py:19
  155.2 7.0 %collective-permute-start.8 = (f32[1,1024]{1,0:T(1,128)S(1)}, f32[1,1024]{1,0:T(1,128)S(1)}, u32[]{:S(2)}, u32[]{:S(2)}) collective-permute-start(f32[1,1024]{1,0:T(1,128)S(1)} %slice.149), channel_id=1, source_target_pairs={{4,0},{8,4},{12,8},{16,12},{20,16},{24,20},{28,24},{5,1},{9,5},{13... | collective-permute-start | bytes 12296 | tf_op jit(solution)/shard_map/ppermute | solution.py:19
  169.8 49.7 %collective-permute-start.11 = (f32[1,512]{1,0:T(1,128)S(1)}, f32[1,512]{1,0:T(1,128)S(1)}, u32[]{:S(2)}, u32[]{:S(2)}) collective-permute-start(f32[1,512]{1,0:T(1,128)S(1)} %bitcast.98), channel_id=1, source_target_pairs={{0,1},{1,2},{2,3},{4,5},{5,6},{6,7},{8,9},{9,10},{10,11},{12,13},{... | collective-permute-start | bytes 6152 | tf_op jit(solution)/shard_map/ppermute | solution.py:19
  174.1 45.6 %collective-permute-start.10 = (f32[1,1024]{1,0:T(1,128)S(1)}, f32[1,1024]{1,0:T(1,128)S(1)}, u32[]{:S(2)}, u32[]{:S(2)}) collective-permute-start(f32[1,1024]{1,0:T(1,128)S(1)} %slice.152), channel_id=1, source_target_pairs={{0,4},{4,8},{8,12},{12,16},{16,20},{20,24},{24,28},{1,5},{5,9},{9,... | collective-permute-start | bytes 12296 | tf_op jit(solution)/shard_map/ppermute | solution.py:19
  219.7 7.5 %copy-start.17 = (f32[512,1024]{1,0:T(8,128)S(1)}, f32[512,1024]{1,0:T(8,128)}, u32[]{:S(2)}) copy-start(f32[512,1024]{1,0:T(8,128)} %copy-done.16) | copy-start | bytes 6291460
  228.6 8.1 %collective-permute-start.13 = (f32[1,512]{1,0:T(1,128)S(1)}, f32[1,512]{1,0:T(1,128)S(1)}, u32[]{:S(2)}, u32[]{:S(2)}) collective-permute-start(f32[1,512]{1,0:T(1,128)S(1)} %bitcast.101), channel_id=1, source_target_pairs={{1,0},{2,1},{3,2},{5,4},{6,5},{7,6},{9,8},{10,9},{11,10},{13,12},{... | collective-permute-start | bytes 6152 | tf_op jit(solution)/shard_map/ppermute | solution.py:19
  229.9 6.9 %collective-permute-start.12 = (f32[1,1024]{1,0:T(1,128)S(1)}, f32[1,1024]{1,0:T(1,128)S(1)}, u32[]{:S(2)}, u32[]{:S(2)}) collective-permute-start(f32[1,1024]{1,0:T(1,128)S(1)} %slice.157), channel_id=1, source_target_pairs={{4,0},{8,4},{12,8},{16,12},{20,16},{24,20},{28,24},{5,1},{9,5},{13... | collective-permute-start | bytes 12296 | tf_op jit(solution)/shard_map/ppermute | solution.py:19
  244.6 48.5 %collective-permute-start.15 = (f32[1,512]{1,0:T(1,128)S(1)}, f32[1,512]{1,0:T(1,128)S(1)}, u32[]{:S(2)}, u32[]{:S(2)}) collective-permute-start(f32[1,512]{1,0:T(1,128)S(1)} %bitcast.96), channel_id=1, source_target_pairs={{0,1},{1,2},{2,3},{4,5},{5,6},{6,7},{8,9},{9,10},{10,11},{12,13},{... | collective-permute-start | bytes 6152 | tf_op jit(solution)/shard_map/ppermute | solution.py:19
  248.9 44.4 %collective-permute-start.14 = (f32[1,1024]{1,0:T(1,128)S(1)}, f32[1,1024]{1,0:T(1,128)S(1)}, u32[]{:S(2)}, u32[]{:S(2)}) collective-permute-start(f32[1,1024]{1,0:T(1,128)S(1)} %slice.160), channel_id=1, source_target_pairs={{0,4},{4,8},{8,12},{12,16},{16,20},{20,24},{24,28},{1,5},{5,9},{9,... | collective-permute-start | bytes 12296 | tf_op jit(solution)/shard_map/ppermute | solution.py:19
  309.0 28.6 %all-to-all-start = ((f32[8,1,1,256,256]{4,3,2,1,0:T(8,128)}), f32[8,1,1,256,256]{4,3,2,1,0:T(8,128)}, u32[]{:S(2)}, u32[]{:S(2)}) async-start(f32[8,1,1,256,256]{4,3,2,1,0:T(8,128)} %fusion.48), calls=%async_computation | async-start | bytes 4194304 | tf_op jit(solution)/shard_map/all_to_all | solution.py:179
  (16 other events, 53.9 us)
where the time goes:
time: 346 us; the launch traced here: 341 us
  blocking collectives  153 us (44%)
  other arithmetic  63.4 us (18%)
  starting transfers between devices  56.2 us (16%)
  local copies, waits for them, and re-layouts  35.1 us (10%)
  waiting for transfers between devices  22.6 us (7%)
  between operations  11.1 us (3%)
    psum x4, blocking collectives, grid_step(): lax.psum((jnp.sum(relaxed * intensity), jnp.sum(relaxed), jnp.sum((1.0 -...  153 us
    ppermute x16, starting transfers between devices, from_behind(): return lax.ppermute(x, axis, pairs)  50.8 us
    all_to_all x1, waiting for transfers between devices, body(): lax.all_to_all(packed, 'rows', split_axis=0, concat_axis=0, tiled=True)  22.5 us
    reduce_sum x3, other arithmetic, grid_step(): jnp.sum(relaxed)  21.3 us
    div x3, other arithmetic, project(): return (trial_down / shrink, trial_right / shrink)  13.1 us
    select_n x2, other arithmetic, grid_step(): new_down = jnp.where(frozen, flux_down, new_down)  12.2 us
    slice x4, local copies, waits for them, and re-layouts, grid_step(): leading[1:]  8.11 us
    select_n x1, other arithmetic, grid_step(): updated = jnp.where(frozen, relaxed, updated)  7.97 us
  transfers between devices with their start and end apart: 17, of which 1 were waited for; matrix products, arithmetic and copies ran while one was open for 6% of the time, Pallas kernels for 0%

commit v1 on v0

v1 whole, which is shorter than its diff:
```python
import functools

import jax
import jax.numpy as jnp
from jax import lax
from jax.experimental import pallas as pl
from jax.experimental.pallas import tpu as pltpu
from jax.sharding import PartitionSpec as P

TILE = 256
ITERS_BEFORE = 2
ITERS_AFTER = 2
ITERS = ITERS_BEFORE + ITERS_AFTER

sigma_step = 0.35
tau_step = 0.35
fidelity = 1.0

SUB = 8
LANES = 128
TOP = 2 * SUB


def kernel(
    n_rows,
    n_cols,
    cost_ref,
    owner_ref,
    i_hbm,
    e_hbm,
    l_hbm,
    out_ref,
    img,
    edge,
    lab,
    u,
    v,
    p1,
    p2,
    wmap,
    colmask,
    rowmask,
    strip_out,
    strip_in,
    part_a,
    got_a,
    part_b,
    got_b,
    tiles,
    pack,
    recv,
    load_sem,
    strip_send,
    strip_recv,
    rim_send,
    rim_recv,
    a_send,
    a_recv,
    b_send,
    b_recv,
    t_send,
    t_recv,
):
    height, width = lab.shape
    wide = img.shape[1]
    tiles_down, tiles_across = height // TILE, width // TILE
    slots = out_ref.shape[0]
    r = lax.axis_index("rows")
    c = lax.axis_index("cols")
    own = pl.ds(TOP, height)
    chunks = height // SUB
    f32 = jnp.float32

    def local(src, dst, k):
        return pltpu.make_async_copy(src, dst, load_sem.at[k])

    loads = [
        local(l_hbm, lab, 0),
        local(i_hbm, img.at[own, pl.ds(0, width)], 1),
        local(e_hbm, edge.at[own, pl.ds(0, width)], 2),
    ]
    for load in loads:
        load.start()

    def row_peer(d):
        return (lax.rem(r + d, n_rows), c)

    def col_peer(d):
        return (r, lax.rem(c + d, n_cols))

    barrier = pltpu.get_barrier_semaphore()
    for d in range(1, n_rows):
        pl.semaphore_signal(barrier, inc=1, device_id=row_peer(d), device_id_type=pl.DeviceIdType.MESH)
    for d in range(1, n_cols):
        pl.semaphore_signal(barrier, inc=1, device_id=col_peer(d), device_id_type=pl.DeviceIdType.MESH)

    def remote(src, dst, send, got, peer):
        return pltpu.make_async_remote_copy(
            src_ref=src, dst_ref=dst, send_sem=send, recv_sem=got,
            device_id=peer, device_id_type=pl.DeviceIdType.MESH,
        )

    lane = lax.broadcasted_iota(jnp.int32, (SUB, LANES), 1)
    sublane = lax.broadcasted_iota(jnp.int32, (SUB, LANES), 0)
    total_bands = n_rows * tiles_down
    total_across = n_cols * tiles_across
    for band in range(tiles_down + 2):
        tr = jnp.clip(r * tiles_down + band - 1, 0, total_bands - 1)
        for t in range(tiles_across):
            w = cost_ref[tr, c * tiles_across + t].astype(f32)
            for h in range(TILE // LANES):
                wmap[band * SUB:(band + 1) * SUB, t * TILE + h * LANES:t * TILE + (h + 1) * LANES] = (
                    jnp.full((SUB, LANES), w * (tau_step * fidelity), f32)
                )
        right = cost_ref[tr, jnp.clip((c + 1) * tiles_across, 0, total_across - 1)].astype(f32)
        left = cost_ref[tr, jnp.clip(c * tiles_across - 1, 0, total_across - 1)].astype(f32)
        wmap[band * SUB:(band + 1) * SUB, width:] = (
            jnp.where(lane < LANES // 2, jnp.full((SUB, LANES), right, f32), jnp.full((SUB, LANES), left, f32))
            * (tau_step * fidelity)
        )
    one = jnp.ones((SUB, LANES), f32)
    last_col = (c == n_cols - 1).astype(f32)
    first_col = (c == 0).astype(f32)
    last_row = (r == n_rows - 1).astype(f32)
    first_row = (r == 0).astype(f32)
    edge_lane = (lane == LANES - 1).astype(f32)
    edge_sub = (sublane == SUB - 1).astype(f32)
    colmask[:, :LANES] = one - edge_lane * last_col
    colmask[:, LANES:] = one - edge_lane * first_col

    def fill_rows(k, _):
        rowmask[pl.ds(k * SUB, SUB), :] = one
        return 0

    lax.fori_loop(0, chunks + 4, fill_rows, 0)
    rowmask[SUB:2 * SUB, :] = one - edge_sub * first_row
    rowmask[TOP + height - SUB:TOP + height, :] = one - edge_sub * last_row
    zero_wide = jnp.zeros((SUB, wide), f32)
    p1[0:SUB, :] = zero_wide
    u[0:SUB, :] = zero_wide
    bottom = slice(TOP + height + SUB, TOP + height + 2 * SUB)
    u[bottom, :] = zero_wide
    v[bottom, :] = zero_wide

    pl.semaphore_wait(barrier, n_rows + n_cols - 2)
    for load in loads:
        load.wait()

    left_cols = slice(0, LANES)
    right_cols = slice(width - LANES, width)
    for side, cols in enumerate((left_cols, right_cols)):
        take = slice(0, SUB) if side == 0 else slice(LANES - SUB, LANES)
        strip_out[side, 0:SUB, :] = lab[:, cols].astype(f32).T[take]
        strip_out[side, SUB:2 * SUB, :] = img[TOP:TOP + height, cols].T[take]
        strip_out[side, 2 * SUB:, :] = edge[TOP:TOP + height, cols].T[take]
    strips = [
        remote(strip_out.at[0], strip_in.at[0], strip_send.at[0], strip_recv.at[0], col_peer(n_cols - 1)),
        remote(strip_out.at[1], strip_in.at[1], strip_send.at[1], strip_recv.at[1], col_peer(1)),
    ]
    for strip in strips:
        strip.start()

    zero = jnp.zeros((SUB, LANES), f32)

    def lane_sum(x):
        total = x[:, :LANES]
        for k in range(1, width // LANES):
            total = total + x[:, k * LANES:(k + 1) * LANES]
        return total

    def add_sums(acc, field, image):
        rest = 1.0 - field
        return (
            acc[0] + lane_sum(field * image),
            acc[1] + lane_sum(field),
            acc[2] + lane_sum(rest * image),
            acc[3] + lane_sum(rest),
        )

    def first(k, acc):
        rows = pl.ds(pl.multiple_of(TOP + k * SUB, SUB), SUB)
        field = lab[pl.ds(pl.multiple_of(k * SUB, SUB), SUB), :].astype(f32)
        u[rows, :width] = field
        return add_sums(acc, field, img[rows, :width])

    acc = lax.fori_loop(0, chunks, first, (zero,) * 4)

    def start_a(it, acc):
        stacked = jnp.concatenate([jnp.sum(x, axis=0, keepdims=True) for x in acc] + [zero[:SUB - 4]], axis=0)
        part_a[it] = stacked
        copies = [
            remote(part_a.at[it], got_a.at[it, d - 1], a_send.at[it, d - 1], a_recv.at[it, d - 1], row_peer(d))
            for d in range(1, n_rows)
        ]
        for copy in copies:
            copy.start()
        return copies

    def start_b(it, copies):
        for copy in copies:
            copy.wait()
        total = part_a[it]
        for d in range(n_rows - 1):
            total = total + got_a[it, d]
        part_b[it] = total
        copies = [
            remote(part_b.at[it], got_b.at[it, d - 1], b_send.at[it, d - 1], b_recv.at[it, d - 1], col_peer(d))
            for d in range(1, n_cols)
        ]
        for copy in copies:
            copy.start()
        return copies

    def means(it, copies):
        for copy in copies:
            copy.wait()
        total = part_b[it]
        for d in range(n_cols - 1):
            total = total + got_b[it, d]
        sums = jnp.sum(total, axis=1, keepdims=True)
        return (sums[0:1] / sums[1:2], sums[2:3] / sums[3:4])

    pending = start_a(0, acc)

    for strip in strips:
        strip.wait()
    middle = jnp.ones((LANES - 2 * SUB, height), f32)
    for k, buf in enumerate((u, img, edge)):
        part = slice(k * SUB, (k + 1) * SUB)
        buf[TOP:TOP + height, width:] = jnp.concatenate(
            [strip_in[0, part, :], middle, strip_in[1, part, :]], axis=0
        ).T
    rims = []
    for k, buf in enumerate((u, img, edge)):
        rims.append(remote(
            buf.at[pl.ds(TOP, SUB)], buf.at[pl.ds(TOP + height, SUB)],
            rim_send.at[2 * k], rim_recv.at[2 * k], row_peer(n_rows - 1)))
        rims.append(remote(
            buf.at[pl.ds(TOP + height - SUB, SUB)], buf.at[pl.ds(TOP - SUB, SUB)],
            rim_send.at[2 * k + 1], rim_recv.at[2 * k + 1], row_peer(1)))
    for rim in rims:
        rim.start()
    for rim in rims:
        rim.wait()

    def band_of(k):
        return (k - 2 + TILE // SUB) // (TILE // SUB)

    def weights(k):
        return wmap[pl.ds(pl.multiple_of(band_of(k) * SUB, SUB), SUB), :]

    wide_sub = lax.broadcasted_iota(jnp.int32, (SUB, wide), 0)

    def dual(it, k):
        base = pl.multiple_of(k * SUB, SUB)
        rows = pl.ds(base, SUB)
        source = u if it == 0 else v
        here = source[rows, :]
        below = source[pl.ds(pl.multiple_of(base + SUB, SUB), SUB), :]
        gx = pltpu.roll(jnp.where(wide_sub == 0, below, here), SUB - 1, 0) - here
        gy = pltpu.roll(here, wide - 1, 1) - here
        if it == 0:
            q1, q2 = gx * sigma_step, gy * sigma_step
        else:
            old1, old2 = p1[rows, :], p2[rows, :]
            q1, q2 = old1 + gx, old2 + gy
        q1 = q1 * jnp.concatenate([rowmask[rows, :]] * (wide // LANES), axis=1)
        cut = width - LANES
        q2 = jnp.concatenate([q2[:, :cut], q2[:, cut:] * colmask[...]], axis=1)
        shrink = jnp.minimum(1.0, edge[rows, :] * lax.rsqrt(q1 * q1 + q2 * q2))
        q1, q2 = q1 * shrink, q2 * shrink
        if it >= ITERS_BEFORE:
            live = weights(k) > 0.0
            q1, q2 = jnp.where(live, q1, old1), jnp.where(live, q2, old2)
        p1[rows, :] = q1
        p2[rows, :] = q2

    def primal(it, k, slope, middle_mean):
        base = pl.multiple_of(k * SUB, SUB)
        rows = pl.ds(base, SUB)
        old = u[rows, :]
        image = img[rows, :]
        here1, here2 = p1[rows, :], p2[rows, :]
        above = p1[pl.ds(pl.multiple_of(base - SUB, SUB), SUB), :]
        shifted = pltpu.roll(jnp.where(wide_sub == SUB - 1, above, here1), 1, 0)
        div = (here1 - shifted) + (here2 - pltpu.roll(here2, 1, 1))
        w = weights(k)
        new = jnp.clip(old + (div * tau_step - w * (slope * (image - middle_mean))), 0.0, 1.0)
        if it >= ITERS_BEFORE:
            new = jnp.where(w > 0.0, new, old)
        return old, new, image, w

    for it in range(ITERS):
        half = chunks // 2 + 2

        def dual_loop(lo, hi):
            def step(k, _):
                dual(it, k)
                return 0
            lax.fori_loop(lo, hi, step, 0)

        dual_loop(1, half)
        pending = start_b(it, pending)
        dual_loop(half, chunks + 3)
        c1, c2 = means(it, pending)
        slope = 2.0 * (c2 - c1)
        middle_mean = 0.5 * (c1 + c2)

        def update(k):
            old, new, image, w = primal(it, k, slope, middle_mean)
            rows = pl.ds(pl.multiple_of(k * SUB, SUB), SUB)
            ahead = new + (new - old)
            if it == ITERS_BEFORE - 1:
                ahead = jnp.where(w > 0.0, ahead, new)
            u[rows, :] = new
            v[rows, :] = ahead * sigma_step
            return new, image

        if it < ITERS - 1:
            update(1)

            def step(k, acc):
                new, image = update(k)
                return add_sums(acc, new[:, :width], image[:, :width])

            acc = lax.fori_loop(2, chunks + 2, step, (zero,) * 4)
            pending = start_a(it + 1, acc)
            update(chunks + 2)
        else:
            def last(k, _):
                new = primal(it, k, slope, middle_mean)[1]
                row = (k - 2) // (TILE // SUB)
                at = pl.ds(pl.multiple_of(lax.rem(k - 2, TILE // SUB) * SUB, SUB), SUB)
                for t in range(tiles_across):
                    tiles[row * tiles_across + t, at, :] = new[:, t * TILE:(t + 1) * TILE]
                return 0

            lax.fori_loop(2, chunks + 2, last, 0)

    own_owner = [
        owner_ref[r * tiles_down + a, c * tiles_across + b]
        for a in range(tiles_down) for b in range(tiles_across)
    ]
    step_rows = 32

    def fill(dst, k):
        source = jnp.int32(0)
        used = jnp.int32(0)
        for t, o in enumerate(own_owner):
            hit = (o >= k * slots) & (o < (k + 1) * slots)
            source = jnp.where(hit, t, source)
            used = jnp.where(hit, 1, used)
        scale = used.astype(f32)

        def step(j, _):
            at = pl.ds(pl.multiple_of(j * step_rows, step_rows), step_rows)
            dst[at, :] = tiles[source, at, :] * scale
            return 0

        lax.fori_loop(0, TILE // step_rows, step, 0)

    sends = []
    for d in list(range(1, n_rows)):
        fill(pack.at[d - 1], lax.rem(r + d, n_rows))
        copy = remote(pack.at[d - 1], recv.at[r], t_send.at[d - 1], t_recv.at[d - 1], row_peer(d))
        copy.start()
        sends.append(copy)
    fill(recv.at[r], r)

    origin = []
    for s in range(slots):
        def look(a, carry):
            source, used = carry
            for b in range(tiles_across):
                hit = owner_ref[a, c * tiles_across + b] == r * slots + s
                source = jnp.where(hit, a // tiles_down, source)
                used = jnp.where(hit, 1, used)
            return source, used
        origin.append(lax.fori_loop(0, total_bands, look, (jnp.int32(0), jnp.int32(0))))

    for copy in sends:
        copy.wait()
    for s in range(slots):
        source, used = origin[s]
        scale = used.astype(f32)

        def step(j, _):
            at = pl.ds(pl.multiple_of(j * step_rows, step_rows), step_rows)
            out_ref[s, 0, at, :] = recv[source, at, :] * scale
            return 0

        lax.fori_loop(0, TILE // step_rows, step, 0)


def body(n_rows, n_cols, intensity, edge_weight, labels, tile_cost, tile_owner):
    height, width = intensity.shape
    tiles_down, tiles_across = height // TILE, width // TILE
    slots = tiles_down * tiles_across // 2
    f32 = jnp.float32
    full = pltpu.VMEM((TOP + height + TOP, width + LANES), f32)
    dma = pltpu.SemaphoreType.DMA
    anywhere = pl.BlockSpec(memory_space=pl.ANY)
    smem = pl.BlockSpec(memory_space=pltpu.SMEM)
    return pl.pallas_call(
        functools.partial(kernel, n_rows, n_cols),
        out_shape=jax.ShapeDtypeStruct((slots, 1, TILE, TILE), f32),
        in_specs=[smem, smem, anywhere, anywhere, anywhere],
        out_specs=pl.BlockSpec(memory_space=pltpu.VMEM),
        scratch_shapes=[
            full,
            full,
            pltpu.VMEM((height, width), jnp.int32),
            full,
            full,
            full,
            full,
            pltpu.VMEM(((tiles_down + 2) * SUB, width + LANES), f32),
            pltpu.VMEM((SUB, 2 * LANES), f32),
            pltpu.VMEM((TOP + height + TOP, LANES), f32),
            pltpu.VMEM((2, 3 * SUB, height), f32),
            pltpu.VMEM((2, 3 * SUB, height), f32),
            pltpu.VMEM((ITERS, SUB, LANES), f32),
            pltpu.VMEM((ITERS, n_rows - 1, SUB, LANES), f32),
            pltpu.VMEM((ITERS, SUB, LANES), f32),
            pltpu.VMEM((ITERS, n_cols - 1, SUB, LANES), f32),
            pltpu.VMEM((tiles_down * tiles_across, TILE, TILE), f32),
            pltpu.VMEM((n_rows - 1, TILE, TILE), f32),
            pltpu.VMEM((n_rows, TILE, TILE), f32),
            dma((3,)),
            dma((2,)),
            dma((2,)),
            dma((6,)),
            dma((6,)),
            dma((ITERS, n_rows - 1)),
            dma((ITERS, n_rows - 1)),
            dma((ITERS, n_cols - 1)),
            dma((ITERS, n_cols - 1)),
            dma((n_rows - 1,)),
            dma((n_rows - 1,)),
        ],
        compiler_params=pltpu.CompilerParams(
            collective_id=0, has_side_effects=True, vmem_limit_bytes=56 * 1024 * 1024
        ),
    )(tile_cost, tile_owner, intensity, edge_weight, labels)


def solution(mesh):
    return jax.shard_map(
        functools.partial(body, mesh.shape["rows"], mesh.shape["cols"]),
        mesh=mesh,
        in_specs=(P("rows", "cols"), P("rows", "cols"), P("rows", "cols"), P(), P()),
        out_specs=P("rows", "cols", None, None),
        check_vma=False,
    )
```

time: 346 us -> 96.2 us (0.28); the launches traced: 341 us -> 95.9 us
  blocking collectives: 153 us -> 0 us
  Pallas kernels: 0 us -> 93.6 us
  other arithmetic: 63.4 us -> 0 us
  starting transfers between devices: 56.2 us -> 0 us
  local copies, waits for them, and re-layouts: 35.1 us -> 2.29 us
  waiting for transfers between devices: 22.6 us -> 0 us
  between operations: 11.1 us -> 0.01 us
    psum x4 -> x0, blocking collectives: 153 us -> none  [grid_step(): lax.psum((jnp.sum(relaxed * intensity), jnp.sum(relaxed), jnp.sum((1.0 -...]
    pallas_call x0 -> x1, Pallas kernels: none -> 93.6 us  [body(): pl.pallas_call(functools.partial(kernel, n_rows, n_cols), out_shape=jax.S...]
    ppermute x16 -> x0, starting transfers between devices: 50.8 us -> none  [from_behind(): return lax.ppermute(x, axis, pairs)]
    all_to_all x1 -> x0, waiting for transfers between devices: 22.5 us -> none  [body(): lax.all_to_all(packed, 'rows', split_axis=0, concat_axis=0, tiled=True)]
    reduce_sum x7 -> x0, other arithmetic: 21.9 us -> none  [the longest x3 21.3 us: grid_step(): jnp.sum(relaxed)]
    select_n x10 -> x0, other arithmetic: 21.5 us -> none  [the longest x2 12.2 us: grid_step(): new_down = jnp.where(frozen, flux_down, new_down)]
    slice x24 -> x0, local copies, waits for them, and re-layouts: 17.5 us -> none  [the longest x4 8.11 us: grid_step(): leading[1:]]
    div x3 -> x0, other arithmetic: 13.1 us -> none  [project(): return (trial_down / shrink, trial_right / shrink)]
  transfers between devices with their start and end apart: 17 -> 0, of which waited for: 1 -> 0; matrix products, arithmetic and copies ran while one was open for 6% -> 0% of each run, Pallas kernels for 0% -> 0%
where the time goes in v1:
time: 96.2 us; the launch traced here: 95.9 us
  Pallas kernels  93.6 us (97%)
  local copies, waits for them, and re-layouts  2.29 us (2%)
    pallas_call x1, Pallas kernels, body(): pl.pallas_call(functools.partial(kernel, n_rows, n_cols), out_shape=jax.S...  93.6 us
    unnamed x1, local copies, waits for them, and re-layouts  2.29 us

profile of v1, /device:TPU:1, one launch (start us, length us, event | category | flops | bytes accessed | tf_op | source)
XLA Modules:
  0.0 95.9 jit_solution(7625266207502137396)
XLA Ops:
  0.0 93.6 %shard_map.55 = f32[4,1,256,256]{3,2,1,0:T(8,128)} custom-call(s32[16,16]{1,0:T(8,128)} %cost_ref.1, s32[16,16]{1,0:T(8,128)} %owner_ref.1, f32[512,1024]{1,0:T(8,128)} %i_hbm.1, f32[512,1024]{1,0:T(8,128)} %e_hbm.1, s32[512,1024]{1,0:T(8,128)} %l_hbm.1), custom_call_target="tpu_custom_call" | custom-call | tf_op jit(solution)/shard_map/pallas_call | solution.py:404
  93.6 2.3 %copy.7 = f32[4,1,256,256]{3,2,1,0:T(8,128)} copy(f32[4,1,256,256]{3,2,1,0:T(8,128)} %shard_map.55) | data formatting | bytes 2097152

commit v2 on v1

--- a/solution.py
+++ b/solution.py
@@ -18,6 +18,7 @@
 
 SUB = 8
 LANES = 128
+BATCH = 4
 TOP = 2 * SUB
 
 
@@ -183,7 +184,7 @@
         u[rows, :width] = field
         return add_sums(acc, field, img[rows, :width])
 
-    acc = lax.fori_loop(0, chunks, first, (zero,) * 4)
+    acc = lax.fori_loop(0, chunks, first, (zero,) * 4, unroll=4)
 
     def start_a(it, acc):
         stacked = jnp.concatenate([jnp.sum(x, axis=0, keepdims=True) for x in acc] + [zero[:SUB - 4]], axis=0)
@@ -251,53 +252,66 @@
 
     wide_sub = lax.broadcasted_iota(jnp.int32, (SUB, wide), 0)
 
-    def dual(it, k):
-        base = pl.multiple_of(k * SUB, SUB)
-        rows = pl.ds(base, SUB)
+    def rows_at(start, j):
+        base = pl.multiple_of(start * SUB, SUB)
+        return pl.ds(pl.multiple_of(base + j * SUB, SUB), SUB)
+
+    def dual(it, start, count):
         source = u if it == 0 else v
-        here = source[rows, :]
-        below = source[pl.ds(pl.multiple_of(base + SUB, SUB), SUB), :]
-        gx = pltpu.roll(jnp.where(wide_sub == 0, below, here), SUB - 1, 0) - here
-        gy = pltpu.roll(here, wide - 1, 1) - here
-        if it == 0:
-            q1, q2 = gx * sigma_step, gy * sigma_step
-        else:
-            old1, old2 = p1[rows, :], p2[rows, :]
-            q1, q2 = old1 + gx, old2 + gy
-        q1 = q1 * jnp.concatenate([rowmask[rows, :]] * (wide // LANES), axis=1)
+        fields = [source[rows_at(start, j), :] for j in range(count + 1)]
         cut = width - LANES
-        q2 = jnp.concatenate([q2[:, :cut], q2[:, cut:] * colmask[...]], axis=1)
-        shrink = jnp.minimum(1.0, edge[rows, :] * lax.rsqrt(q1 * q1 + q2 * q2))
-        q1, q2 = q1 * shrink, q2 * shrink
-        if it >= ITERS_BEFORE:
-            live = weights(k) > 0.0
-            q1, q2 = jnp.where(live, q1, old1), jnp.where(live, q2, old2)
-        p1[rows, :] = q1
-        p2[rows, :] = q2
-
-    def primal(it, k, slope, middle_mean):
-        base = pl.multiple_of(k * SUB, SUB)
-        rows = pl.ds(base, SUB)
-        old = u[rows, :]
-        image = img[rows, :]
-        here1, here2 = p1[rows, :], p2[rows, :]
-        above = p1[pl.ds(pl.multiple_of(base - SUB, SUB), SUB), :]
-        shifted = pltpu.roll(jnp.where(wide_sub == SUB - 1, above, here1), 1, 0)
-        div = (here1 - shifted) + (here2 - pltpu.roll(here2, 1, 1))
-        w = weights(k)
-        new = jnp.clip(old + (div * tau_step - w * (slope * (image - middle_mean))), 0.0, 1.0)
-        if it >= ITERS_BEFORE:
-            new = jnp.where(w > 0.0, new, old)
-        return old, new, image, w
+        results = []
+        for j in range(count):
+            rows = rows_at(start, j)
+            here = fields[j]
+            gx = pltpu.roll(jnp.where(wide_sub == 0, fields[j + 1], here), SUB - 1, 0) - here
+            gy = pltpu.roll(here, wide - 1, 1) - here
+            if it == 0:
+                q1, q2 = gx * sigma_step, gy * sigma_step
+            else:
+                old1, old2 = p1[rows, :], p2[rows, :]
+                q1, q2 = old1 + gx, old2 + gy
+            q1 = q1 * jnp.concatenate([rowmask[rows, :]] * (wide // LANES), axis=1)
+            q2 = jnp.concatenate([q2[:, :cut], q2[:, cut:] * colmask[...]], axis=1)
+            shrink = jnp.minimum(1.0, edge[rows, :] * lax.rsqrt(q1 * q1 + q2 * q2))
+            q1, q2 = q1 * shrink, q2 * shrink
+            if it >= ITERS_BEFORE:
+                live = weights(start + j) > 0.0
+                q1, q2 = jnp.where(live, q1, old1), jnp.where(live, q2, old2)
+            results.append((q1, q2))
+        for j, (q1, q2) in enumerate(results):
+            p1[rows_at(start, j), :] = q1
+            p2[rows_at(start, j), :] = q2
+
+    def primal(it, start, count, slope, middle_mean):
+        duals = [p1[rows_at(start, j), :] for j in range(-1, count)]
+        results = []
+        for j in range(count):
+            rows = rows_at(start, j)
+            old = u[rows, :]
+            image = img[rows, :]
+            here1, here2 = duals[j + 1], p2[rows, :]
+            shifted = pltpu.roll(jnp.where(wide_sub == SUB - 1, duals[j], here1), 1, 0)
+            div = (here1 - shifted) + (here2 - pltpu.roll(here2, 1, 1))
+            w = weights(start + j)
+            new = jnp.clip(old + (div * tau_step - w * (slope * (image - middle_mean))), 0.0, 1.0)
+            if it >= ITERS_BEFORE:
+                new = jnp.where(w > 0.0, new, old)
+            results.append((old, new, image, w))
+        return results
 
     for it in range(ITERS):
         half = chunks // 2 + 2
 
         def dual_loop(lo, hi):
+            whole = (hi - lo) // BATCH
+
             def step(k, _):
-                dual(it, k)
+                dual(it, lo + k * BATCH, BATCH)
                 return 0
-            lax.fori_loop(lo, hi, step, 0)
+            lax.fori_loop(0, whole, step, 0)
+            if lo + whole * BATCH < hi:
+                dual(it, lo + whole * BATCH, hi - lo - whole * BATCH)
 
         dual_loop(1, half)
         pending = start_b(it, pending)
@@ -306,36 +320,39 @@
         slope = 2.0 * (c2 - c1)
         middle_mean = 0.5 * (c1 + c2)
 
-        def update(k):
-            old, new, image, w = primal(it, k, slope, middle_mean)
-            rows = pl.ds(pl.multiple_of(k * SUB, SUB), SUB)
-            ahead = new + (new - old)
-            if it == ITERS_BEFORE - 1:
-                ahead = jnp.where(w > 0.0, ahead, new)
-            u[rows, :] = new
-            v[rows, :] = ahead * sigma_step
-            return new, image
+        def update(start, count):
+            results = primal(it, start, count, slope, middle_mean)
+            for j, (old, new, image, w) in enumerate(results):
+                ahead = new + (new - old)
+                if it == ITERS_BEFORE - 1:
+                    ahead = jnp.where(w > 0.0, ahead, new)
+                u[rows_at(start, j), :] = new
+                v[rows_at(start, j), :] = ahead * sigma_step
+            return results
 
         if it < ITERS - 1:
-            update(1)
+            update(1, 1)
 
             def step(k, acc):
-                new, image = update(k)
-                return add_sums(acc, new[:, :width], image[:, :width])
-
-            acc = lax.fori_loop(2, chunks + 2, step, (zero,) * 4)
+                for _, new, image, _ in update(2 + k * BATCH, BATCH):
+                    acc = add_sums(acc, new[:, :width], image[:, :width])
+                return acc
+
+            acc = lax.fori_loop(0, chunks // BATCH, step, (zero,) * 4)
             pending = start_a(it + 1, acc)
-            update(chunks + 2)
+            update(chunks + 2, 1)
         else:
             def last(k, _):
-                new = primal(it, k, slope, middle_mean)[1]
-                row = (k - 2) // (TILE // SUB)
-                at = pl.ds(pl.multiple_of(lax.rem(k - 2, TILE // SUB) * SUB, SUB), SUB)
-                for t in range(tiles_across):
-                    tiles[row * tiles_across + t, at, :] = new[:, t * TILE:(t + 1) * TILE]
+                results = primal(it, 2 + k * BATCH, BATCH, slope, middle_mean)
+                per_tile = TILE // SUB // BATCH
+                row = k // per_tile
+                for j, (_, new, _, _) in enumerate(results):
+                    at = pl.ds(pl.multiple_of(lax.rem(k, per_tile) * (BATCH * SUB) + j * SUB, SUB), SUB)
+                    for t in range(tiles_across):
+                        tiles[row * tiles_across + t, at, :] = new[:, t * TILE:(t + 1) * TILE]
                 return 0
 
-            lax.fori_loop(2, chunks + 2, last, 0)
+            lax.fori_loop(0, chunks // BATCH, last, 0)
 
     own_owner = [
         owner_ref[r * tiles_down + a, c * tiles_across + b]

time: 96.2 us -> 79.1 us (0.82)
  Pallas kernels: 93.6 us -> 76.6 us
    pallas_call x1, Pallas kernels: 93.6 us -> 76.6 us  [body(): pl.pallas_call(functools.partial(kernel, n_rows, n_cols), out_shape=jax.S...]
where the time goes in v2:
time: 79.1 us; the launch traced here: 78.9 us
  Pallas kernels  76.6 us (97%)
  local copies, waits for them, and re-layouts  2.29 us (3%)
    pallas_call x1, Pallas kernels, body(): pl.pallas_call(functools.partial(kernel, n_rows, n_cols), out_shape=jax.S...  76.6 us
    unnamed x1, local copies, waits for them, and re-layouts  2.29 us

profile of v2, /device:TPU:1, one launch (start us, length us, event | category | flops | bytes accessed | tf_op | source)
XLA Modules:
  0.0 78.9 jit_solution(16586515421973769044)
XLA Ops:
  0.0 76.6 %shard_map.55 = f32[4,1,256,256]{3,2,1,0:T(8,128)} custom-call(s32[16,16]{1,0:T(8,128)} %cost_ref.1, s32[16,16]{1,0:T(8,128)} %owner_ref.1, f32[512,1024]{1,0:T(8,128)} %i_hbm.1, f32[512,1024]{1,0:T(8,128)} %e_hbm.1, s32[512,1024]{1,0:T(8,128)} %l_hbm.1), custom_call_target="tpu_custom_call" | custom-call | tf_op jit(solution)/shard_map/pallas_call | solution.py:421
  76.6 2.3 %copy.7 = f32[4,1,256,256]{3,2,1,0:T(8,128)} copy(f32[4,1,256,256]{3,2,1,0:T(8,128)} %shard_map.55) | data formatting | bytes 2097152

commit v3 on v2

--- a/solution.py
+++ b/solution.py
@@ -38,6 +38,7 @@
     v,
     p1,
     p2,
+    moved,
     wmap,
     colmask,
     rowmask,
@@ -279,22 +280,29 @@
                 live = weights(start + j) > 0.0
                 q1, q2 = jnp.where(live, q1, old1), jnp.where(live, q2, old2)
             results.append((q1, q2))
+        before = p1[rows_at(start, -1), :]
+        ahead = []
         for j, (q1, q2) in enumerate(results):
-            p1[rows_at(start, j), :] = q1
-            p2[rows_at(start, j), :] = q2
+            shifted = pltpu.roll(jnp.where(wide_sub == SUB - 1, before, q1), 1, 0)
+            div = (q1 - shifted) + (q2 - pltpu.roll(q2, 1, 1))
+            old = fields[j] if it == 0 else u[rows_at(start, j), :]
+            ahead.append(old + div * tau_step)
+            before = q1
+        for j, (q1, q2) in enumerate(results):
+            rows = rows_at(start, j)
+            p1[rows, :] = q1
+            if it < ITERS - 1:
+                p2[rows, :] = q2
+            moved[rows, :] = ahead[j]
 
     def primal(it, start, count, slope, middle_mean):
-        duals = [p1[rows_at(start, j), :] for j in range(-1, count)]
         results = []
         for j in range(count):
             rows = rows_at(start, j)
             old = u[rows, :]
             image = img[rows, :]
-            here1, here2 = duals[j + 1], p2[rows, :]
-            shifted = pltpu.roll(jnp.where(wide_sub == SUB - 1, duals[j], here1), 1, 0)
-            div = (here1 - shifted) + (here2 - pltpu.roll(here2, 1, 1))
             w = weights(start + j)
-            new = jnp.clip(old + (div * tau_step - w * (slope * (image - middle_mean))), 0.0, 1.0)
+            new = jnp.clip(moved[rows, :] - w * (slope * (image - middle_mean)), 0.0, 1.0)
             if it >= ITERS_BEFORE:
                 new = jnp.where(w > 0.0, new, old)
             results.append((old, new, image, w))
@@ -427,6 +435,7 @@
             full,
             full,
             pltpu.VMEM((height, width), jnp.int32),
+            full,
             full,
             full,
             full,

time: 79.1 us -> 75.2 us (0.951)
  Pallas kernels: 76.6 us -> 72.6 us
    pallas_call x1, Pallas kernels: 76.6 us -> 72.6 us  [body(): pl.pallas_call(functools.partial(kernel, n_rows, n_cols), out_shape=jax.S...]
where the time goes in v3:
time: 75.2 us; the launch traced here: 74.9 us
  Pallas kernels  72.6 us (97%)
  local copies, waits for them, and re-layouts  2.29 us (3%)
    pallas_call x1, Pallas kernels, body(): pl.pallas_call(functools.partial(kernel, n_rows, n_cols), out_shape=jax.S...  72.6 us
    unnamed x1, local copies, waits for them, and re-layouts  2.29 us

profile of v3, /device:TPU:1, one launch (start us, length us, event | category | flops | bytes accessed | tf_op | source)
XLA Modules:
  0.0 74.9 jit_solution(8212007655797335617)
XLA Ops:
  0.0 72.6 %shard_map.55 = f32[4,1,256,256]{3,2,1,0:T(8,128)} custom-call(s32[16,16]{1,0:T(8,128)} %cost_ref.1, s32[16,16]{1,0:T(8,128)} %owner_ref.1, f32[512,1024]{1,0:T(8,128)} %i_hbm.1, f32[512,1024]{1,0:T(8,128)} %e_hbm.1, s32[512,1024]{1,0:T(8,128)} %l_hbm.1), custom_call_target="tpu_custom_call" | custom-call | tf_op jit(solution)/shard_map/pallas_call | solution.py:429
  72.6 2.3 %copy.7 = f32[4,1,256,256]{3,2,1,0:T(8,128)} copy(f32[4,1,256,256]{3,2,1,0:T(8,128)} %shard_map.55) | data formatting | bytes 2097152
